TPU v7x, 32 devices: a whole 2x2x4 slice. The times are simulated.
32 devices in a mesh: head: 4 (over y, x), blk: 8 (over z, core).
Axes of the slice: x: 2, y: 2, z: 4, core: 2. Of those that a mesh axis runs over, the one named last changes fastest.
Arguments:
- hidden_in: bfloat16 [2048, 4096], P(('blk', 'head')), may hold values from -6 to 6
- queries: bfloat16 [2048, 2048], P(('blk', 'head')), may hold values from -26 to 26
- key_states: bfloat16 [2048, 1024], P(('blk', 'head')), may hold values from -5 to 5
- value_states: bfloat16 [2048, 1024], P(('blk', 'head')), may hold values from -6 to 6
- out_weight: bfloat16 [2048, 4096], P('head'), may hold values from -0.125 to 0.125
- norm_gain: float32 [4096], replicated, may hold values from 0.1 to 1.9
- gate_weight: bfloat16 [4096, 7168], P(None, 'head'), may hold values from -0.09375 to 0.09375
- up_weight: bfloat16 [4096, 7168], P(None, 'head'), may hold values from -0.09375 to 0.09375
- down_weight: bfloat16 [7168, 4096], P('head'), may hold values from -0.0625 to 0.0625
Outputs:
- layer_out: bfloat16 [2048, 4096], P(('blk', 'head'))
All inputs are finite; a program needn't handle non-finite values.
Results may differ from a plain program's by a relative error of at most 0.018.
Values may be sent and summed in bfloat16 or wider, within the bound.
A program may use at most 192 MiB of HBM per device.

v0:
```python
import jax
import jax.numpy as jnp
from jax import lax
from jax.sharding import PartitionSpec as P

HEADS = 16
KV_HEADS = 8
HEAD_DIM = 128
negative_fill = -1e30


def absorb_rows(running, query_groups, query_pos, key_block, value_block, key_pos):
    row_peak, row_total, weighted = running
    key_count = key_block.shape[0]
    group_count = query_groups.shape[1]
    head_size = query_groups.shape[3]
    key_heads = key_block.reshape(key_count, group_count, head_size)
    value_heads = value_block.reshape(key_count, group_count, head_size)
    scores = jnp.einsum(
        "qgrd,kgd->grqk", query_groups, key_heads, preferred_element_type=jnp.float32
    ) * head_size ** (-0.5)
    visible = key_pos[None, :] <= query_pos[:, None]
    new_peak = jnp.maximum(row_peak, jnp.max(jnp.where(visible, scores, negative_fill), axis=-1))
    exp_scores = jnp.where(visible, jnp.exp(scores - new_peak[..., None]), 0.0)
    new_total = jnp.sum(exp_scores, axis=-1)
    products = jnp.einsum(
        "grqk,kgd->grqd",
        exp_scores.astype(jnp.bfloat16),
        value_heads,
        preferred_element_type=jnp.float32,
    )
    return (new_peak, new_total, products)


def local(
    hidden_in,
    queries,
    key_states,
    value_states,
    out_weight,
    norm_gain,
    gate_weight,
    up_weight,
    down_weight,
):
    own_block = lax.axis_index("blk")
    query_local, key_local, value_local = (
        lax.all_to_all(queries, "head", split_axis=1, concat_axis=0, tiled=True),
        lax.all_to_all(key_states, "head", split_axis=1, concat_axis=0, tiled=True),
        lax.all_to_all(value_states, "head", split_axis=1, concat_axis=0, tiled=True),
    )
    block_rows = query_local.shape[0]
    query_width = query_local.shape[1]
    key_width = key_local.shape[1]
    group_count = key_width // HEAD_DIM
    group_ratio = HEADS // KV_HEADS
    local_index = jnp.arange(block_rows, dtype=jnp.int32)
    start_state = (
        jnp.full((group_count, group_ratio, block_rows), negative_fill, jnp.float32),
        jnp.zeros((group_count, group_ratio, block_rows), jnp.float32),
        jnp.zeros((group_count, group_ratio, block_rows, HEAD_DIM), jnp.float32),
    )
    query_pos = own_block * block_rows + local_index
    query_groups = query_local.reshape(block_rows, group_count, group_ratio, HEAD_DIM)
    last_query = own_block * block_rows + block_rows - 1
    key_block = lax.all_gather(key_local, "blk", axis=0, tiled=True)
    value_block = lax.all_gather(value_local, "blk", axis=0, tiled=True)
    key_pos = jnp.arange(key_block.shape[0], dtype=jnp.int32)

    def skipped(state):
        return state

    def worked(state):
        return absorb_rows(state, query_groups, query_pos, key_block, value_block, key_pos)

    row_peak, row_total, weighted = lax.cond(
        jnp.int32(0) > last_query, skipped, worked, start_state
    )
    attended = (
        (weighted / row_total[..., None])
        .transpose(2, 0, 1, 3)
        .reshape(block_rows, query_width)
        .astype(jnp.bfloat16)
    )
    selected = attended
    projected = lax.psum_scatter(
        jnp.dot(selected, out_weight, preferred_element_type=jnp.float32).astype(jnp.bfloat16),
        "head",
        scatter_dimension=0,
        tiled=True,
    ).astype(jnp.float32)
    residual = (hidden_in.astype(jnp.float32) + projected).astype(jnp.bfloat16)
    widened = residual.astype(jnp.float32)
    mean_square = jnp.mean(widened * widened, axis=-1, keepdims=True)
    normed = (widened * lax.rsqrt(mean_square + 1e-05) * norm_gain).astype(jnp.bfloat16)
    shard_rows = lax.all_gather(normed, "head", axis=0, tiled=True)
    gate_part = jnp.dot(shard_rows, gate_weight, preferred_element_type=jnp.float32)
    up_part = jnp.dot(shard_rows, up_weight, preferred_element_type=jnp.float32)
    inner_act = (jax.nn.silu(gate_part) * up_part).astype(jnp.bfloat16)
    selected = inner_act
    mlp_out = lax.psum_scatter(
        jnp.dot(selected, down_weight, preferred_element_type=jnp.float32).astype(jnp.bfloat16),
        "head",
        scatter_dimension=0,
        tiled=True,
    ).astype(jnp.float32)
    return (residual.astype(jnp.float32) + mlp_out).astype(jnp.bfloat16)


def solution(mesh):
    return jax.shard_map(
        local,
        mesh=mesh,
        in_specs=(
            P(("blk", "head"), None),
            P(("blk", "head"), None),
            P(("blk", "head"), None),
            P(("blk", "head"), None),
            P("head", None),
            P(),
            P(None, "head"),
            P(None, "head"),
            P("head", None),
        ),
        out_specs=P(("blk", "head"), None),
        check_vma=False,
    )
```

profile of v0, /device:TPU:0, one launch (start us, length us, event | category | flops | bytes accessed | tf_op | source)
XLA Modules:
  0.0 231.0 jit_solution(15140094676042932576)
XLA Ops:
  6.5 0.0 all-gather.4.cloned.1.call-start
  6.5 0.9 copy.59
  7.5 10.1 %all_to_all.54 = bf16[64,4,256]{2,0,1:T(8,128)(2,1)} all-to-all(bf16[64,4,256]{2,0,1:T(8,128)(2,1)S(1)} %bitcast.51), channel_id=1, replica_groups=mesh['head'=4,'blk'=8] {'head'}, dimensions={1} | all-to-all | bytes 262144 | tf_op jit(solution)/shard_map/all_to_all | solution.py:49
  17.6 0.0 all-gather.4.cloned.1.call-update
  17.6 0.0 all-gather.6.cloned.1.call-start
  17.6 0.9 copy.58
  18.6 8.1 %all_to_all.55 = bf16[64,4,256]{2,0,1:T(8,128)(2,1)} all-to-all(bf16[64,4,256]{2,0,1:T(8,128)(2,1)S(1)} %bitcast.52), channel_id=1, replica_groups=mesh['head'=4,'blk'=8] {'head'}, dimensions={1} | all-to-all | bytes 262144 | tf_op jit(solution)/shard_map/all_to_all | solution.py:50
  26.6 0.0 all-gather.6.cloned.1.call-update
  26.7 1.7 copy.57
  28.3 3.4 %all-to-all-start.1 = ((bf16[64,4,512]{2,0,1:T(8,128)(2,1)}), bf16[64,4,512]{2,0,1:T(8,128)(2,1)S(1)}, u32[]{:S(2)}, u32[]{:S(2)}) async-start(bf16[64,4,512]{2,0,1:T(8,128)(2,1)} %bitcast.42), calls=%async_computation.1 | async-start | bytes 524288 | tf_op jit(solution)/shard_map/all_to_all | solution.py:48
  31.8 0.0 reduce-scatter.3.cloned.1.call-start
  31.8 5.3 %all-to-all-done.1 = bf16[64,4,512]{2,0,1:T(8,128)(2,1)S(1)} async-done(((bf16[64,4,512]{2,0,1:T(8,128)(2,1)}), bf16[64,4,512]{2,0,1:T(8,128)(2,1)S(1)}, u32[]{:S(2)}, u32[]{:S(2)}) %all-to-all-start.1) | async-done | bytes 262176 | tf_op jit(solution)/shard_map/all_to_all | solution.py:48
  37.1 2.6 %all-gather.4.cloned.1.call-done = bf16[2048,256]{1,0:T(8,128)(2,1)} async-done(((bf16[256,256]{1,0:T(8,128)(2,1)}), bf16[2048,256]{1,0:T(8,128)(2,1)}) %all-gather.4.cloned.1.call-update) | async-done | bytes 1048592 | tf_op jit(solution)/shard_map/all_gather | solution.py:66
  39.7 23.5 %all-gather.6.cloned.1.call-done = bf16[2048,256]{1,0:T(8,128)(2,1)} async-done(((bf16[256,256]{1,0:T(8,128)(2,1)}), bf16[2048,256]{1,0:T(8,128)(2,1)}) %all-gather.6.cloned.1.call-update) | async-done | bytes 1048592 | tf_op jit(solution)/shard_map/all_gather | solution.py:67
  63.2 14.5 %conditional.1 = (f32[2,2,256]{2,1,0:T(2,128)S(1)}, f32[2,2,256,128]{2,3,1,0:T(8,128)S(1)}) conditional(s32[]{:T(128)} %convert_element_type.47, (s32[2048]{0:T(1024)S(1)}, s32[]{:T(128)}, s32[256]{0:T(256)S(1)}, bf16[2048,256]{1,0:T(8,128)(2,1)}, bf16[4,64,512]{2,1,0:T(8,128)(2,1)S(1)}, /*index=5*/bf16[2048,256]{1,0:T(8,128)(2,1)}) %tuple.31, () %tuple.14), branch_computations={%region_0.3_spmd, %region_3.4_spmd} | conditional | flops 1097334016 | bytes 72649808 | solution.py:76
  63.2 0.4 broadcast_compare_fusion
  63.6 1.3 reshape.34
  65.0 0.1 reshape.35
  65.1 0.0 copy-start.3
  65.1 4.7 %fusion = (f32[2,2,256]{2,1,0:T(2,128)S(1)}, f32[2,2048,256,2]{2,1,3,0:T(8,128)}) fusion(pred[256,2048]{0,1:T(8,128)(4,1)S(1)} %broadcast_compare_fusion, bf16[256,2,2,128]{3,2,1,0:T(2,128)(2,1)S(1)} %reshape.35, bf16[2048,2,128,1]{2,1,0,3:T(2,128)(2,1)S(1)} %bitcast.46), kind=kOutput, calls=%fused_computation.2 | convolution fusion | flops 543161344 | bytes 10227712 | tf_op jit(solution)/shard_map/cond/branch_0_fun/qgrd,kgd->grqk/dot_general | solution.py:19
  69.8 0.0 copy-done.3
  69.8 0.3 reshape.36
  70.1 0.0 copy-start
  70.1 5.3 %fusion.5 = f32[2,2,256,128]{2,3,1,0:T(8,128)S(1)} fusion(f32[2,2048,256,2]{2,1,3,0:T(8,128)} %get-tuple-element.38, f32[2,2,256]{2,1,0:T(2,128)S(1)} %broadcast_maximum_fusion, pred[256,2048]{0,1:T(8,128)(4,1)S(1)} %broadcast_compare_fusion, bf16[2048,2,128,1]{2,1,0,3:T(2,128)(2,1)S(1)} %bitcast.47), kind=kOutput, calls=%fused_computation.7 | convolution fusion | flops 545259520 | bytes 10489856 | tf_op jit(solution)/shard_map/cond | solution.py:76
  75.4 0.4 copy-done
  75.8 1.8 fusion.4
  77.7 0.0 copy-start.1
  77.7 0.0 copy-start.4
  77.7 4.9 %convolution_convert_fusion.1 = bf16[256,4096]{1,0:T(8,128)(2,1)} fusion(bf16[256,512]{0,1:T(8,128)(2,1)S(1)} %bitcast.45, bf16[512,4096]{1,0:T(8,128)(2,1)} %param.15), kind=kOutput, calls=%fused_computation.19 | convolution fusion | flops 1074790400 | bytes 6553600 | tf_op jit(solution)/shard_map/dot_general | solution.py:87
  82.6 0.0 reduce-scatter.3.cloned.1.call-update
  82.6 0.0 all-gather.8.cloned.1.call-start
  82.7 34.9 %reduce-scatter.3.cloned.1.call-done = bf16[64,4096]{1,0:T(8,128)(2,1)} async-done(((bf16[256,4096]{1,0:T(8,128)(2,1)}), bf16[64,4096]{1,0:T(8,128)(2,1)}) %reduce-scatter.3.cloned.1.call-update) | async-done | bytes 524304 | tf_op jit(solution)/shard_map/reduce_scatter | solution.py:86
  117.6 0.0 copy-done.1
  117.6 1.3 fusion.15
  118.9 0.0 copy-done.4
  118.9 2.0 fusion.17
  120.9 0.0 all-gather.8.cloned.1.call-update
  121.0 0.2 reduce-scatter.5.cloned.1.call-start
  121.2 35.1 %all-gather.8.cloned.1.call-done = bf16[256,4096]{1,0:T(8,128)(2,1)} async-done(((bf16[64,4096]{1,0:T(8,128)(2,1)}), bf16[256,4096]{1,0:T(8,128)(2,1)}) %all-gather.8.cloned.1.call-update) | async-done | bytes 2097168 | tf_op jit(solution)/shard_map/all_gather | solution.py:96
  156.3 0.0 copy-start.5
  156.3 11.1 %fusion.20 = f32[256,1792]{1,0:T(8,128)} fusion(bf16[256,4096]{1,0:T(8,128)(2,1)} %all-gather.8.cloned.1.call-done, bf16[4096,1792]{1,0:T(8,128)(2,1)} %param.17), kind=kOutput, calls=%fused_computation.36 | convolution fusion | flops 3758096384 | bytes 18612224 | tf_op jit(solution)/shard_map/dot_general | solution.py:97
  167.4 0.0 copy-done.5
  167.4 0.0 copy-start.2
  167.4 19.6 %convolution_convert_fusion = bf16[256,4096]{1,0:T(8,128)(2,1)} fusion(bf16[1792,4096]{1,0:T(8,128)(2,1)} %param.19, bf16[256,4096]{1,0:T(8,128)(2,1)S(1)} %copy-done.5, bf16[4096,1792]{1,0:T(8,128)(2,1)} %param.18, f32[256,1792]{1,0:T(8,128)} %fusion.20), kind=kOutput, calls=%fused_computation.18 | convolution fusion | flops 7519993856 | bytes 35389440 | tf_op jit(solution)/shard_map/dot_general | solution.py:102
  187.0 0.0 reduce-scatter.5.cloned.1.call-update
  187.1 35.3 %reduce-scatter.5.cloned.1.call-done = bf16[64,4096]{1,0:T(8,128)(2,1)} async-done(((bf16[256,4096]{1,0:T(8,128)(2,1)}), bf16[64,4096]{1,0:T(8,128)(2,1)}) %reduce-scatter.5.cloned.1.call-update) | async-done | bytes 524304 | tf_op jit(solution)/shard_map/reduce_scatter | solution.py:101
  222.4 0.0 copy-done.2
  222.4 2.0 fusion.18
  (6 shorter events, 0.1 us)
Async XLA Ops:
  6.5 33.2 %all-gather.4.cloned.1.call-start = ((), (), s32[]{:S(2)}) async-start(), calls=%async_computation.5 | async-start | bytes 1179648 | tf_op jit(solution)/shard_map/all_gather | solution.py:66
  17.6 45.6 %all-gather.6.cloned.1.call-start = ((), (), s32[]{:S(2)}) async-start(), calls=%async_computation.6 | async-start | bytes 1179648 | tf_op jit(solution)/shard_map/all_gather | solution.py:67
  28.3 8.8 %all-to-all-start.1 = ((bf16[64,4,512]{2,0,1:T(8,128)(2,1)}), bf16[64,4,512]{2,0,1:T(8,128)(2,1)S(1)}, u32[]{:S(2)}, u32[]{:S(2)}) async-start(bf16[64,4,512]{2,0,1:T(8,128)(2,1)} %bitcast.42), calls=%async_computation.1 | async-start | bytes 524288 | tf_op jit(solution)/shard_map/all_to_all | solution.py:48
  31.8 85.8 %reduce-scatter.3.cloned.1.call-start = ((), (), s32[]{:S(2)}) async-start(), calls=%async_computation.7 | async-start | bytes 2621440 | tf_op jit(solution)/shard_map/reduce_scatter | solution.py:86
  65.1 4.7 %copy-start.3 = (bf16[2048,256]{1,0:T(8,128)(2,1)S(1)}, bf16[2048,256]{1,0:T(8,128)(2,1)}, u32[]{:S(2)}) copy-start(bf16[2048,256]{1,0:T(8,128)(2,1)} %get-tuple-element.25) | copy-start | bytes 3145732 | tf_op jit(solution)/shard_map/cond
  70.1 5.8 %copy-start = (f32[2,2048,256,2]{2,1,3,0:T(8,128)S(1)}, f32[2,2048,256,2]{2,1,3,0:T(8,128)}, u32[]{:S(2)}) copy-start(f32[2,2048,256,2]{2,1,3,0:T(8,128)} %get-tuple-element.38) | copy-start | bytes 25165828 | tf_op jit(solution)/shard_map/cond
  77.7 39.8 %copy-start.1 = (bf16[64,4096]{1,0:T(8,128)(2,1)S(1)}, bf16[64,4096]{1,0:T(8,128)(2,1)}, u32[]{:S(2)}) copy-start(bf16[64,4096]{1,0:T(8,128)(2,1)} %param.11) | copy-start | bytes 1572868
  77.7 41.2 %copy-start.4 = (f32[4096]{0:T(1024)S(1)}, f32[4096]{0:T(1024)}, u32[]{:S(2)}) copy-start(f32[4096]{0:T(1024)} %param.16) | copy-start | bytes 49156
  82.6 73.7 %all-gather.8.cloned.1.call-start = ((), (), s32[]{:S(2)}) async-start(), calls=%async_computation.8 | async-start | bytes 2621440 | tf_op jit(solution)/shard_map/all_gather | solution.py:96
  121.0 101.4 %reduce-scatter.5.cloned.1.call-start = ((), (), s32[]{:S(2)}) async-start(), calls=%async_computation.9 | async-start | bytes 2621440 | tf_op jit(solution)/shard_map/reduce_scatter | solution.py:101
  156.3 11.1 %copy-start.5 = (bf16[256,4096]{1,0:T(8,128)(2,1)S(1)}, bf16[256,4096]{1,0:T(8,128)(2,1)}, u32[]{:S(2)}) copy-start(bf16[256,4096]{1,0:T(8,128)(2,1)} %all-gather.8.cloned.1.call-done) | copy-start | bytes 6291460
  167.4 55.0 %copy-start.2 = (bf16[64,4096]{1,0:T(8,128)(2,1)S(1)}, bf16[64,4096]{1,0:T(8,128)(2,1)}, u32[]{:S(2)}) copy-start(bf16[64,4096]{1,0:T(8,128)(2,1)} %reduce-scatter.3.cloned.1.call-done) | copy-start | bytes 1572868
Sparse Core Ops, SparseCore 0:
  17.7 21.9 all-gather.3
  41.3 21.8 all-gather.5
  82.7 34.7 reduce-scatter.2
  121.1 35.1 all-gather.7
  187.2 35.1 reduce-scatter.4
where the time goes:
time: 231 us
  waiting for transfers between devices  137 us (59%)
  matrix products  45.6 us (20%)
  blocking collectives  18.2 us (8%)
  between operations  13.2 us (6%)
  other arithmetic  7.69 us (3%)
  local copies, waits for them, and re-layouts  5.68 us (2%)
  starting transfers between devices  3.76 us (2%)
    reduce_scatter x1, waiting for transfers between devices, local(): lax.psum_scatter(jnp.dot(selected, down_weight, preferred_element_type=jn...  35.3 us
    all_gather x1, waiting for transfers between devices, local(): shard_rows = lax.all_gather(normed, 'head', axis=0, tiled=True)  35.1 us
    reduce_scatter x1, waiting for transfers between devices, local(): lax.psum_scatter(jnp.dot(selected, out_weight, preferred_element_type=jnp...  34.9 us
    all_gather x1, waiting for transfers between devices, local(): value_block = lax.all_gather(value_local, 'blk', axis=0, tiled=True)  23.5 us
    dot_general x1, matrix products, local(): jnp.dot(selected, down_weight, preferred_element_type=jnp.float32)  19.6 us
    dot_general x1, matrix products, local(): jnp.dot(shard_rows, gate_weight, preferred_element_type=jnp.float32)  11.1 us
    all_to_all x1, blocking collectives, local(): lax.all_to_all(key_states, 'head', split_axis=1, concat_axis=0, tiled=True)  10.1 us
    all_to_all x1, blocking collectives, local(): lax.all_to_all(value_states, 'head', split_axis=1, concat_axis=0, tiled=T...  8.07 us
  transfers between devices with their start and end apart: 6, of which 6 were waited for; matrix products, arithmetic and copies ran while one was open for 1% of the time, Pallas kernels for 0%

commit v1 on v0

--- a/solution.py
+++ b/solution.py
@@ -64,7 +64,12 @@
     query_groups = query_local.reshape(block_rows, group_count, group_ratio, HEAD_DIM)
     last_query = own_block * block_rows + block_rows - 1
     key_block = lax.all_gather(key_local, "blk", axis=0, tiled=True)
-    value_block = lax.all_gather(value_local, "blk", axis=0, tiled=True)
+    ring = [value_local]
+    for hop in range(7):
+        ring.append(lax.ppermute(ring[-1], "blk", [(dev, (dev + 1) % 8) for dev in range(8)]))
+    value_block = jnp.roll(
+        jnp.concatenate(ring[::-1], axis=0), (lax.axis_index("blk") + 1) * ring[0].shape[0], axis=0
+    )
     key_pos = jnp.arange(key_block.shape[0], dtype=jnp.int32)
 
     def skipped(state):

time: 231 us -> 257 us (1.11)
  waiting for transfers between devices: 137 us -> 160 us
  local copies, waits for them, and re-layouts: 5.68 us -> 19.6 us
  blocking collectives: 18.2 us -> 10 us
  matrix products: 45.6 us -> 38.9 us
  starting transfers between devices: 3.76 us -> 7.09 us
    ppermute x0 -> x7, waiting for transfers between devices: none -> 37.1 us  [local(): lax.ppermute(ring[-1], 'blk', [(dev, (dev + 1) % 8) for dev in range(8)])]
    all_gather x1 -> x0, waiting for transfers between devices: 23.5 us -> none  [local(): value_block = lax.all_gather(value_local, 'blk', axis=0, tiled=True)]
    all_gather x1, waiting for transfers between devices: 2.61 us -> 13.5 us  [local(): key_block = lax.all_gather(key_local, 'blk', axis=0, tiled=True)]
    all_to_all x1 -> x0, blocking collectives: 10.1 us -> none  [local(): lax.all_to_all(key_states, 'head', split_axis=1, concat_axis=0, tiled=True)]
    unnamed x8 -> x25, local copies, waits for them, and re-layouts: 0.02 us -> 9.98 us
    all_to_all x1, waiting for transfers between devices: 5.28 us -> 0.01 us  [local(): lax.all_to_all(queries, 'head', split_axis=1, concat_axis=0, tiled=True)]
    cond x1, matrix products: 5.31 us -> 1.91 us  [local(): lax.cond(jnp.int32(0) > last_query, skipped, worked, start_state)]
    all_to_all x0 -> x1, starting transfers between devices: none -> 3.32 us  [local(): lax.all_to_all(key_states, 'head', split_axis=1, concat_axis=0, tiled=True)]
  transfers between devices with their start and end apart: 6 -> 13, of which waited for: 6 -> 11; matrix products, arithmetic and copies ran while one was open for 1% -> 5% of each run, Pallas kernels for 0% -> 0%
where the time goes in v1:
time: 257 us
  waiting for transfers between devices  160 us (62%)
  matrix products  38.9 us (15%)
  local copies, waits for them, and re-layouts  19.6 us (8%)
  between operations  13.2 us (5%)
  blocking collectives  10 us (4%)
  other arithmetic  7.73 us (3%)
  starting transfers between devices  7.09 us (3%)
    ppermute x7, waiting for transfers between devices, local(): lax.ppermute(ring[-1], 'blk', [(dev, (dev + 1) % 8) for dev in range(8)])  37.1 us
    reduce_scatter x1, waiting for transfers between devices, local(): lax.psum_scatter(jnp.dot(selected, down_weight, preferred_element_type=jn...  35.3 us
    all_gather x1, waiting for transfers between devices, local(): shard_rows = lax.all_gather(normed, 'head', axis=0, tiled=True)  35.1 us
    reduce_scatter x1, waiting for transfers between devices, local(): lax.psum_scatter(jnp.dot(selected, out_weight, preferred_element_type=jnp...  34.9 us
    dot_general x1, matrix products, local(): jnp.dot(selected, down_weight, preferred_element_type=jnp.float32)  19.6 us
    all_gather x1, waiting for transfers between devices, local(): key_block = lax.all_gather(key_local, 'blk', axis=0, tiled=True)  13.5 us
    dot_general x1, matrix products, local(): jnp.dot(shard_rows, gate_weight, preferred_element_type=jnp.float32)  11.1 us
    all_to_all x1, blocking collectives, local(): lax.all_to_all(value_states, 'head', split_axis=1, concat_axis=0, tiled=T...  10 us
  transfers between devices with their start and end apart: 13, of which 11 were waited for; matrix products, arithmetic and copies ran while one was open for 5% of the time, Pallas kernels for 0%

profile of v1, /device:TPU:0, one launch (start us, length us, event | category | flops | bytes accessed | tf_op | source)
XLA Modules:
  0.0 256.6 jit_solution(10637949514280151439)
XLA Ops:
  6.5 0.9 copy.73
  7.5 10.0 %all_to_all.54 = bf16[64,4,256]{2,0,1:T(8,128)(2,1)S(1)} all-to-all(bf16[64,4,256]{2,0,1:T(8,128)(2,1)S(1)} %bitcast.58), channel_id=1, replica_groups=mesh['head'=4,'blk'=8] {'head'}, dimensions={1} | all-to-all | bytes 262144 | tf_op jit(solution)/shard_map/all_to_all | solution.py:50
  17.5 0.0 collective-permute-start
  17.5 6.2 %collective-permute-done = bf16[256,256]{1,0:T(8,128)(2,1)S(1)} collective-permute-done((bf16[256,256]{1,0:T(8,128)(2,1)S(1)}, bf16[256,256]{1,0:T(8,128)(2,1)S(1)}, u32[]{:S(2)}, u32[]{:S(2)}) %collective-permute-start) | collective-permute-done | bytes 131104 | tf_op jit(solution)/shard_map/ppermute | solution.py:69
  23.7 0.0 collective-permute-start.1
  23.7 6.2 %collective-permute-done.1 = bf16[256,256]{1,0:T(8,128)(2,1)S(1)} collective-permute-done((bf16[256,256]{1,0:T(8,128)(2,1)S(1)}, bf16[256,256]{1,0:T(8,128)(2,1)S(1)}, u32[]{:S(2)}, u32[]{:S(2)}) %collective-permute-start.1) | collective-permute-done | bytes 131104 | tf_op jit(solution)/shard_map/ppermute | solution.py:69
  29.8 0.0 collective-permute-start.2
  29.9 6.2 %collective-permute-done.2 = bf16[256,256]{1,0:T(8,128)(2,1)S(1)} collective-permute-done((bf16[256,256]{1,0:T(8,128)(2,1)S(1)}, bf16[256,256]{1,0:T(8,128)(2,1)S(1)}, u32[]{:S(2)}, u32[]{:S(2)}) %collective-permute-start.2) | collective-permute-done | bytes 131104 | tf_op jit(solution)/shard_map/ppermute | solution.py:69
  36.0 0.0 collective-permute-start.3
  36.0 6.2 %collective-permute-done.3 = bf16[256,256]{1,0:T(8,128)(2,1)S(1)} collective-permute-done((bf16[256,256]{1,0:T(8,128)(2,1)S(1)}, bf16[256,256]{1,0:T(8,128)(2,1)S(1)}, u32[]{:S(2)}, u32[]{:S(2)}) %collective-permute-start.3) | collective-permute-done | bytes 131104 | tf_op jit(solution)/shard_map/ppermute | solution.py:69
  42.2 0.0 collective-permute-start.4
  42.2 6.2 %collective-permute-done.4 = bf16[256,256]{1,0:T(8,128)(2,1)S(1)} collective-permute-done((bf16[256,256]{1,0:T(8,128)(2,1)S(1)}, bf16[256,256]{1,0:T(8,128)(2,1)S(1)}, u32[]{:S(2)}, u32[]{:S(2)}) %collective-permute-start.4) | collective-permute-done | bytes 131104 | tf_op jit(solution)/shard_map/ppermute | solution.py:69
  48.4 0.0 collective-permute-start.5
  48.4 6.2 %collective-permute-done.5 = bf16[256,256]{1,0:T(8,128)(2,1)S(1)} collective-permute-done((bf16[256,256]{1,0:T(8,128)(2,1)S(1)}, bf16[256,256]{1,0:T(8,128)(2,1)S(1)}, u32[]{:S(2)}, u32[]{:S(2)}) %collective-permute-start.5) | collective-permute-done | bytes 131104 | tf_op jit(solution)/shard_map/ppermute | solution.py:69
  54.6 1.6 copy.74
  56.2 3.3 %all-to-all-start = ((bf16[64,4,256]{2,0,1:T(8,128)(2,1)}), bf16[64,4,256]{2,0,1:T(8,128)(2,1)S(1)}, u32[]{:S(2)}, u32[]{:S(2)}) async-start(bf16[64,4,256]{2,0,1:T(8,128)(2,1)} %bitcast.49), calls=%async_computation | async-start | bytes 262144 | tf_op jit(solution)/shard_map/all_to_all | solution.py:49
  59.5 1.7 copy.72
  61.2 3.3 %all-to-all-done = bf16[64,4,256]{2,0,1:T(8,128)(2,1)S(1)} async-done(((bf16[64,4,256]{2,0,1:T(8,128)(2,1)}), bf16[64,4,256]{2,0,1:T(8,128)(2,1)S(1)}, u32[]{:S(2)}, u32[]{:S(2)}) %all-to-all-start) | async-done | bytes 131104 | tf_op jit(solution)/shard_map/all_to_all | solution.py:49
  64.5 3.4 %all-to-all-start.1 = ((bf16[64,4,512]{2,0,1:T(8,128)(2,1)}), bf16[64,4,512]{2,0,1:T(8,128)(2,1)S(1)}, u32[]{:S(2)}, u32[]{:S(2)}) async-start(bf16[64,4,512]{2,0,1:T(8,128)(2,1)} %bitcast.47), calls=%async_computation.1 | async-start | bytes 524288 | tf_op jit(solution)/shard_map/all_to_all | solution.py:48
  67.9 0.0 all-gather.3.cloned.1.call-start
  68.0 0.7 all-gather.3.cloned.1.call-update
  68.7 0.0 reduce-scatter.3.cloned.1.call-start
  68.7 0.0 collective-permute-done.6
  68.7 0.7 constant_dynamic-update-slice_fusion.15
  69.4 0.6 constant_dynamic-update-slice_fusion.14
  70.0 0.7 constant_dynamic-update-slice_fusion.13
  70.7 0.7 constant_dynamic-update-slice_fusion.12
  71.4 0.7 constant_dynamic-update-slice_fusion.11
  72.0 0.7 constant_dynamic-update-slice_fusion.10
  72.7 0.7 constant_dynamic-update-slice_fusion.9
  73.4 0.7 constant_dynamic-update-slice_fusion.8
  74.0 0.7 constant_dynamic-update-slice_fusion.7
  74.7 0.7 constant_dynamic-update-slice_fusion.6
  75.4 0.7 constant_dynamic-update-slice_fusion.5
  76.0 0.7 constant_dynamic-update-slice_fusion.4
  76.7 0.7 constant_dynamic-update-slice_fusion.3
  77.4 0.7 constant_dynamic-update-slice_fusion.2
  78.0 0.7 constant_dynamic-update-slice_fusion.1
  78.7 0.7 constant_dynamic-update-slice_fusion
  79.4 0.0 all-to-all-done.1
  79.4 13.5 %all-gather.3.cloned.1.call-done = bf16[2048,256]{1,0:T(8,128)(2,1)} async-done(((bf16[256,256]{1,0:T(8,128)(2,1)}), bf16[2048,256]{1,0:T(8,128)(2,1)}) %all-gather.3.cloned.1.call-update) | async-done | bytes 1048592 | tf_op jit(solution)/shard_map/all_gather | solution.py:66
  92.8 10.5 %conditional.1 = (f32[2,2,256]{2,1,0:T(2,128)S(1)}, f32[2,2,256,128]{2,3,1,0:T(8,128)S(1)}) conditional(s32[]{:T(128)} %convert_element_type.50, (s32[2048]{0:T(1024)S(1)}, s32[]{:T(128)}, s32[256]{0:T(256)S(1)}, bf16[2048,256]{1,0:T(8,128)(2,1)}, bf16[4,64,512]{2,1,0:T(8,128)(2,1)S(1)}, /*index=5*/s32[]{:T(128)}, s32[]{:T(128)}, ...), branch_computations={%region_0.3_spmd.clone, %region_3.4_spmd} | conditional | flops 1097334016 | bytes 39095468 | solution.py:81
  92.8 2.9 %copy.47 = bf16[4096,256]{0,1:T(8,128)(2,1)S(1)} copy(bf16[4096,256]{1,0:T(8,128)(2,1)} %get-tuple-element.192) | data formatting | bytes 4194304 | tf_op jit(solution)/shard_map
  95.8 0.4 constant_dynamic-slice_fusion
  96.2 0.1 reshape.48
  96.3 0.5 broadcast_compare_fusion
  96.7 1.3 reshape.47
  98.1 1.5 fusion
  99.6 1.9 fusion.5
  101.5 1.8 fusion.4
  103.4 4.8 %convolution_convert_fusion.1 = bf16[256,4096]{1,0:T(8,128)(2,1)} fusion(bf16[256,512]{0,1:T(8,128)(2,1)S(1)} %bitcast.53, bf16[512,4096]{1,0:T(8,128)(2,1)} %param.15), kind=kOutput, calls=%fused_computation.19 | convolution fusion | flops 1074790400 | bytes 6553600 | tf_op jit(solution)/shard_map/dot_general | solution.py:92
  108.2 0.0 reduce-scatter.3.cloned.1.call-update
  108.2 0.0 all-gather.5.cloned.1.call-start
  108.3 34.9 %reduce-scatter.3.cloned.1.call-done = bf16[64,4096]{1,0:T(8,128)(2,1)} async-done(((bf16[256,4096]{1,0:T(8,128)(2,1)}), bf16[64,4096]{1,0:T(8,128)(2,1)}) %reduce-scatter.3.cloned.1.call-update) | async-done | bytes 524304 | tf_op jit(solution)/shard_map/reduce_scatter | solution.py:91
  143.2 1.3 fusion.14
  144.5 2.0 fusion.16
  146.6 0.0 all-gather.5.cloned.1.call-update
  146.6 0.2 reduce-scatter.5.cloned.1.call-start
  146.8 35.1 %all-gather.5.cloned.1.call-done = bf16[256,4096]{1,0:T(8,128)(2,1)} async-done(((bf16[64,4096]{1,0:T(8,128)(2,1)}), bf16[256,4096]{1,0:T(8,128)(2,1)}) %all-gather.5.cloned.1.call-update) | async-done | bytes 2097168 | tf_op jit(solution)/shard_map/all_gather | solution.py:101
  182.0 11.1 %fusion.19 = f32[256,1792]{1,0:T(8,128)} fusion(bf16[256,4096]{1,0:T(8,128)(2,1)} %all-gather.5.cloned.1.call-done, bf16[4096,1792]{1,0:T(8,128)(2,1)} %param.17), kind=kOutput, calls=%fused_computation.52 | convolution fusion | flops 3758096384 | bytes 18612224 | tf_op jit(solution)/shard_map/dot_general | solution.py:102
  193.1 19.6 %convolution_convert_fusion = bf16[256,4096]{1,0:T(8,128)(2,1)} fusion(bf16[1792,4096]{1,0:T(8,128)(2,1)} %param.19, bf16[256,4096]{1,0:T(8,128)(2,1)S(1)} %copy-done.4, bf16[4096,1792]{1,0:T(8,128)(2,1)} %param.18, f32[256,1792]{1,0:T(8,128)} %fusion.19), kind=kOutput, calls=%fused_computation.18 | convolution fusion | flops 7519993856 | bytes 35389440 | tf_op jit(solution)/shard_map/dot_general | solution.py:107
  212.7 0.0 reduce-scatter.5.cloned.1.call-update
  212.7 35.3 %reduce-scatter.5.cloned.1.call-done = bf16[64,4096]{1,0:T(8,128)(2,1)} async-done(((bf16[256,4096]{1,0:T(8,128)(2,1)}), bf16[64,4096]{1,0:T(8,128)(2,1)}) %reduce-scatter.5.cloned.1.call-update) | async-done | bytes 524304 | tf_op jit(solution)/shard_map/reduce_scatter | solution.py:106
  248.0 2.0 fusion.17
  (17 shorter events, 0.1 us)
Async XLA Ops:
  17.5 6.2 %collective-permute-start = (bf16[256,256]{1,0:T(8,128)(2,1)S(1)}, bf16[256,256]{1,0:T(8,128)(2,1)S(1)}, u32[]{:S(2)}, u32[]{:S(2)}) collective-permute-start(bf16[256,256]{1,0:T(8,128)(2,1)S(1)} %bitcast.50), channel_id=1, source_target_pairs={{0,1},{1,2},{2,3},{3,4},{4,5},{5,6},{6,7},{7,0},{8,9},{9,10},{10,1... | collective-permute-start | bytes 393224 | tf_op jit(solution)/shard_map/ppermute | solution.py:69
  23.7 6.2 %collective-permute-start.1 = (bf16[256,256]{1,0:T(8,128)(2,1)S(1)}, bf16[256,256]{1,0:T(8,128)(2,1)S(1)}, u32[]{:S(2)}, u32[]{:S(2)}) collective-permute-start(bf16[256,256]{1,0:T(8,128)(2,1)S(1)} %collective-permute-done), channel_id=1, source_target_pairs={{0,1},{1,2},{2,3},{3,4},{4,5},{5,6},{6,7},{7,0},{8,9},{9,10},{10,1... | collective-permute-start | bytes 393224 | tf_op jit(solution)/shard_map/ppermute | solution.py:69
  29.8 6.2 %collective-permute-start.2 = (bf16[256,256]{1,0:T(8,128)(2,1)S(1)}, bf16[256,256]{1,0:T(8,128)(2,1)S(1)}, u32[]{:S(2)}, u32[]{:S(2)}) collective-permute-start(bf16[256,256]{1,0:T(8,128)(2,1)S(1)} %collective-permute-done.1), channel_id=1, source_target_pairs={{0,1},{1,2},{2,3},{3,4},{4,5},{5,6},{6,7},{7,0},{8,9},{9,10},{10,1... | collective-permute-start | bytes 393224 | tf_op jit(solution)/shard_map/ppermute | solution.py:69
  36.0 6.2 %collective-permute-start.3 = (bf16[256,256]{1,0:T(8,128)(2,1)S(1)}, bf16[256,256]{1,0:T(8,128)(2,1)S(1)}, u32[]{:S(2)}, u32[]{:S(2)}) collective-permute-start(bf16[256,256]{1,0:T(8,128)(2,1)S(1)} %collective-permute-done.2), channel_id=1, source_target_pairs={{0,1},{1,2},{2,3},{3,4},{4,5},{5,6},{6,7},{7,0},{8,9},{9,10},{10,1... | collective-permute-start | bytes 393224 | tf_op jit(solution)/shard_map/ppermute | solution.py:69
  42.2 6.2 %collective-permute-start.4 = (bf16[256,256]{1,0:T(8,128)(2,1)S(1)}, bf16[256,256]{1,0:T(8,128)(2,1)S(1)}, u32[]{:S(2)}, u32[]{:S(2)}) collective-permute-start(bf16[256,256]{1,0:T(8,128)(2,1)S(1)} %collective-permute-done.3), channel_id=1, source_target_pairs={{0,1},{1,2},{2,3},{3,4},{4,5},{5,6},{6,7},{7,0},{8,9},{9,10},{10,1... | collective-permute-start | bytes 393224 | tf_op jit(solution)/shard_map/ppermute | solution.py:69
  48.4 6.2 %collective-permute-start.5 = (bf16[256,256]{1,0:T(8,128)(2,1)S(1)}, bf16[256,256]{1,0:T(8,128)(2,1)S(1)}, u32[]{:S(2)}, u32[]{:S(2)}) collective-permute-start(bf16[256,256]{1,0:T(8,128)(2,1)S(1)} %collective-permute-done.4), channel_id=1, source_target_pairs={{0,1},{1,2},{2,3},{3,4},{4,5},{5,6},{6,7},{7,0},{8,9},{9,10},{10,1... | collective-permute-start | bytes 393224 | tf_op jit(solution)/shard_map/ppermute | solution.py:69
  54.6 14.1 %collective-permute-start.6 = (bf16[256,256]{1,0:T(8,128)(2,1)S(1)}, bf16[256,256]{1,0:T(8,128)(2,1)S(1)}, u32[]{:S(2)}, u32[]{:S(2)}) collective-permute-start(bf16[256,256]{1,0:T(8,128)(2,1)S(1)} %collective-permute-done.5), channel_id=1, source_target_pairs={{0,1},{1,2},{2,3},{3,4},{4,5},{5,6},{6,7},{7,0},{8,9},{9,10},{10,1... | collective-permute-start | bytes 393224 | tf_op jit(solution)/shard_map/ppermute | solution.py:69
  56.2 8.3 %all-to-all-start = ((bf16[64,4,256]{2,0,1:T(8,128)(2,1)}), bf16[64,4,256]{2,0,1:T(8,128)(2,1)S(1)}, u32[]{:S(2)}, u32[]{:S(2)}) async-start(bf16[64,4,256]{2,0,1:T(8,128)(2,1)} %bitcast.49), calls=%async_computation | async-start | bytes 262144 | tf_op jit(solution)/shard_map/all_to_all | solution.py:49
  64.5 3.5 %copy-start.2 = (bf16[64,4,256]{2,0,1:T(8,128)(2,1)}, bf16[64,4,256]{2,0,1:T(8,128)(2,1)S(1)}, u32[]{:S(2)}) copy-start(bf16[64,4,256]{2,0,1:T(8,128)(2,1)S(1)} %all-to-all-done) | copy-start | bytes 393220
  64.5 14.8 %all-to-all-start.1 = ((bf16[64,4,512]{2,0,1:T(8,128)(2,1)}), bf16[64,4,512]{2,0,1:T(8,128)(2,1)S(1)}, u32[]{:S(2)}, u32[]{:S(2)}) async-start(bf16[64,4,512]{2,0,1:T(8,128)(2,1)} %bitcast.47), calls=%async_computation.1 | async-start | bytes 524288 | tf_op jit(solution)/shard_map/all_to_all | solution.py:48
  67.9 24.9 %all-gather.3.cloned.1.call-start = ((), (), s32[]{:S(2)}) async-start(), calls=%async_computation.5 | async-start | bytes 1179648 | tf_op jit(solution)/shard_map/all_gather | solution.py:66
  68.7 74.5 %reduce-scatter.3.cloned.1.call-start = ((), (), s32[]{:S(2)}) async-start(), calls=%async_computation.6 | async-start | bytes 2621440 | tf_op jit(solution)/shard_map/reduce_scatter | solution.py:91
  108.2 35.0 %copy-start = (bf16[64,4096]{1,0:T(8,128)(2,1)S(1)}, bf16[64,4096]{1,0:T(8,128)(2,1)}, u32[]{:S(2)}) copy-start(bf16[64,4096]{1,0:T(8,128)(2,1)} %param.11) | copy-start | bytes 1572868
  108.2 36.3 %copy-start.3 = (f32[4096]{0:T(1024)S(1)}, f32[4096]{0:T(1024)}, u32[]{:S(2)}) copy-start(f32[4096]{0:T(1024)} %param.16) | copy-start | bytes 49156
  108.2 73.7 %all-gather.5.cloned.1.call-start = ((), (), s32[]{:S(2)}) async-start(), calls=%async_computation.7 | async-start | bytes 2621440 | tf_op jit(solution)/shard_map/all_gather | solution.py:101
  146.6 101.4 %reduce-scatter.5.cloned.1.call-start = ((), (), s32[]{:S(2)}) async-start(), calls=%async_computation.8 | async-start | bytes 2621440 | tf_op jit(solution)/shard_map/reduce_scatter | solution.py:106
  181.9 11.1 %copy-start.4 = (bf16[256,4096]{1,0:T(8,128)(2,1)S(1)}, bf16[256,4096]{1,0:T(8,128)(2,1)}, u32[]{:S(2)}) copy-start(bf16[256,4096]{1,0:T(8,128)(2,1)} %all-gather.5.cloned.1.call-done) | copy-start | bytes 6291460
  212.7 35.4 %copy-start.1 = (bf16[64,4096]{1,0:T(8,128)(2,1)S(1)}, bf16[64,4096]{1,0:T(8,128)(2,1)}, u32[]{:S(2)}) copy-start(bf16[64,4096]{1,0:T(8,128)(2,1)} %reduce-scatter.3.cloned.1.call-done) | copy-start | bytes 1572868
Sparse Core Ops, SparseCore 0:
  70.3 22.4 all-gather.2
  108.4 34.8 reduce-scatter.2
  146.7 35.1 all-gather.4
  212.8 35.1 reduce-scatter.4
